TPU v7x, 32 devices: a whole 2x2x4 slice. The times are simulated.
32 devices in a mesh: stream: 32 (over z, y, x, core), item: 1.
Axes of the slice: x: 2, y: 2, z: 4, core: 2. Of those that a mesh axis runs over, the one named last changes fastest.
Arguments:
- event_items: int32 [131072], P('stream'), may hold values from 0 to 262143, as said below
- event_sessions: int32 [131072], P('stream'), may hold values from 0 to 8191, never falling along the last dimension, each value on 1 to 64 neighbouring positions
- sketch_bits: int32 [15, 262144], P(None, 'item'), may hold values from 0 to 262143
Outputs:
- sketch: float32 [128, 256], P('stream')
Inputs may be any that keep to these rules, and one draw needn't show every extreme that they name: `event_items`: item 262144 - 1 occurs at least once.
All inputs are finite; a program needn't handle non-finite values.
Results may differ from a plain program's by a relative error of at most 0.0006.
Values may be sent and summed in bfloat16 or wider, within the bound.
A program may use at most 128 MiB of HBM per device.

v0:
```python
import functools
import math

import jax
import jax.numpy as jnp
from jax import lax
from jax.experimental import pallas as pl
from jax.experimental.pallas import tpu as pltpu
from jax.sharding import PartitionSpec as P

WINDOW = 15
ITEM_BITS = 18
LANES = 128
BITS_PER_WORD = 18
PLANE = 8
VMEM_GRANT = 45 * 1024 * 1024
NT = (((1,), (1,)), ((), ()))
VMEM = pl.BlockSpec(memory_space=pltpu.VMEM)


def one_where(mask):
    return jnp.where(mask, 1.0, 0.0).astype(jnp.bfloat16)


def hot_columns(ids, values):
    row = jnp.broadcast_to(values, (16, values.shape[1])).astype(jnp.bfloat16)
    one, zero = jnp.ones((), jnp.bfloat16), jnp.zeros((), jnp.bfloat16)
    return jnp.concatenate(
        [jnp.where(ids[n : n + 16] == row, one, zero) for n in range(0, ids.shape[0], 16)], axis=0
    )


def greet_all(slabs, me):
    barrier = pltpu.get_barrier_semaphore()

    for k in range(1, slabs):
        pl.semaphore_signal(
            barrier, inc=1, device_id={"stream": lax.rem(me + k, slabs)}, device_id_type=pl.DeviceIdType.MESH
        )
    return barrier


def send(src, dst, send_sem, recv_sem, to):
    return pltpu.make_async_remote_copy(
        src_ref=src,
        dst_ref=dst,
        send_sem=send_sem,
        recv_sem=recv_sem,
        device_id={"stream": to},
        device_id_type=pl.DeviceIdType.MESH,
    )


def each(low, high, do):
    for k in range(low, high):
        do(k)


def exchange(slabs, me, out_ref, in_ref, send_sems, recv_sems, start):
    def copy(k):
        to = lax.rem(me + k, slabs)
        return send(out_ref.at[to], in_ref.at[me], send_sems.at[k], recv_sems.at[k], to)

    if start:
        each(1, slabs, lambda k: copy(k).start())
        in_ref[me] = out_ref[me]
    else:
        each(1, slabs, lambda k: copy(k).wait())


def gather_kernel(
    slabs, rows, blocks, own_ref, bits_ref, all_ref, head_ref, sign_ref,
    own_pack, own_bits, item_ref, session_ref, links_ref, total_ref,
    pair_out, pair_in, plane_out, plane_in, line_out, line_in,
    bit_sem, line_send, line_recv, plane_send, plane_recv, near_send, near_recv,
    pair_sems, head_plane_send, head_plane_recv, head_line_send, head_line_recv,
):
    me = lax.axis_index("stream")
    depth = slabs // PLANE
    layer, low = me // PLANE, lax.rem(me, PLANE)
    parity, quad = lax.rem(me, 2), lax.rem(me // 2, 4)

    def flip(bit):
        return bit - 2 * bit * lax.rem(me // bit, 2)

    partner = me + flip(1)
    steps = (flip(2), flip(4), flip(2) + flip(4))
    def other_layer(k):
        rising = k + (k - layer + depth) // depth
        mirrored = depth - 1 - layer
        falling = depth - 1 - k - (k - mirrored + depth) // depth
        high = layer // ((depth + 1) // 2)
        return rising + (falling - rising) * lax.rem(high, 2)

    others = [other_layer(k) for k in range(depth - 1)]
    own_items, own_sessions = own_ref.at[0], own_ref.at[1]
    barrier = pltpu.get_barrier_semaphore()
    owned = own_bits.shape[1]
    bit_copy = pltpu.make_async_copy(
        bits_ref.at[:, pl.ds(pl.multiple_of(me * owned, owned), owned)], own_bits, bit_sem.at[0]
    )
    bit_copy.start()
    greeted = [partner] + [me + step for step in steps] + [o * PLANE + low for o in others]
    for to in greeted:
        pl.semaphore_signal(
            barrier, inc=1, device_id={"stream": to}, device_id_type=pl.DeviceIdType.MESH
        )
    half = blocks // 2
    own_pack[0:blocks] = own_items[...]
    own_pack[blocks : blocks + half] = own_sessions[0:half] | (own_sessions[half:blocks] << 16)
    all_ref[me] = own_pack[...]
    item_ref[8 : 8 + blocks] = own_items[...]
    session_ref[8 : 8 + blocks] = own_sessions[...]
    for edge in (slice(0, 8), slice(8 + blocks, 16 + blocks)):
        item_ref[edge] = jnp.zeros((8, LANES), jnp.int32)
        session_ref[edge] = jnp.full((8, LANES), -1, jnp.int32)
    sub = lax.broadcasted_iota(jnp.int32, (LANES, LANES), 0)
    lane = lax.broadcasted_iota(jnp.int32, (LANES, LANES), 1)
    low_lane = lax.broadcasted_iota(jnp.int32, (1, LANES), 1) < LANES // 2
    ids = lax.broadcasted_iota(jnp.int32, (rows, LANES), 0)
    gaps = (sub - LANES // 2 - lane, sub + LANES // 2 - lane)
    in_reach = [(jnp.abs(gap) <= WINDOW) & (gap != 0) for gap in gaps]
    ones = jnp.ones((8, 2 * LANES), jnp.float32).astype(jnp.bfloat16)
    links_ref[...] = jnp.zeros_like(links_ref)
    total_ref[...] = jnp.zeros_like(total_ref)

    def block(b, unused):
        def around(ref):
            turned = [pltpu.roll(ref[pl.ds(b + o, 1)], LANES // 2, 1) for o in (7, 8, 9)]
            return (
                jnp.where(low_lane, turned[0], turned[1]),
                jnp.where(low_lane, turned[1], turned[2]),
            )

        own_item, own_session = item_ref[pl.ds(b + 8, 1)], session_ref[pl.ds(b + 8, 1)]
        hot = jnp.concatenate([one_where(ids == item) for item in around(item_ref)], axis=1)
        linked = jnp.concatenate(
            [
                one_where((jnp.broadcast_to(session, (LANES, LANES)).T == own_session) & reach)
                for session, reach in zip(around(session_ref), in_reach)
            ],
            axis=0,
        )
        links = jnp.dot(jnp.concatenate([hot, ones], axis=0), linked, preferred_element_type=jnp.float32)
        links_ref[...] += lax.dot_general(
            links.astype(jnp.bfloat16), one_where(ids == own_item), NT, preferred_element_type=jnp.float32
        )
        total_ref[...] += links[rows:]
        return unused

    inner = [blocks * n // 32 for n in (0, 16, 32)]

    def blocks_of(n):
        lax.fori_loop(inner[n], inner[n + 1], block, 0, unroll=4)

    step_columns = max(LANES, owned // 16)
    steps_in_all = owned // step_columns

    def signs(low_step, high_step):
        def step(t, unused):
            at = pl.multiple_of(t * step_columns, step_columns)
            sign_ref[:, pl.ds(at, step_columns)] = sign_table(own_bits[:, pl.ds(at, step_columns)], sign_ref.shape[0])
            return unused

        lax.fori_loop(low_step * steps_in_all // 16, high_step * steps_in_all // 16, step, 0)

    blocks_of(0)
    bit_copy.wait()
    pl.semaphore_wait(barrier, len(greeted))

    def along_line(there, here):
        return send(
            own_pack, all_ref.at[me], line_send.at[there], line_recv.at[here], there * PLANE + low
        )

    def in_plane(d, at_layer, own=False):
        slab = all_ref.at[at_layer * PLANE + low]
        sem = d * depth + at_layer
        return send(own_pack if own else slab, slab, plane_send.at[sem], plane_recv.at[sem], me + steps[d])

    def to_partner(r, at_layer, own=False):
        slab = all_ref.at[at_layer * PLANE + low + ((0,) + steps)[r]]
        sem = r * depth + at_layer
        return send(own_pack if own else slab, slab, near_send.at[sem], near_recv.at[sem], partner)

    for o in reversed(others):
        along_line(o, layer).start()
    for d in range(3):
        in_plane(d, layer, True).start()
    to_partner(0, layer, True).start()

    def forward_line(k):
        along_line(layer, others[k]).wait_recv()
        for d in range(3):
            in_plane(d, others[k]).start()
        to_partner(0, others[k]).start()

    def forward_plane(at_layer):
        for d in range(3):
            in_plane(d, at_layer).wait_recv()
            to_partner(d + 1, at_layer).start()

    blocks_of(1)
    share = rows // slabs
    tail = jnp.concatenate(
        [links_ref[rows : rows + 1], total_ref[0:1], jnp.zeros((6 - share, LANES), jnp.float32)], axis=0
    )
    for d in range(slabs):
        at = (d % 2, d // PLANE, d // 2 % 4)
        pair_out[at + (slice(0, share),)] = links_ref[d * share : (d + 1) * share]
        pair_out[at + (slice(share, 8),)] = tail

    pair = send(pair_out.at[1 - parity], pair_in, pair_sems.at[0], pair_sems.at[1], partner)
    pair.start()
    signs(0, 2)
    forward_line(0)
    pair.wait()
    line_out[...] = pair_out[parity] + pair_in[...]

    def head_line(there, here):
        return send(
            line_out.at[there], line_in.at[layer], head_line_send.at[there], head_line_recv.at[here],
            there * PLANE + low,
        )

    for o in others:
        head_line(o, layer).start()
    line_in[layer] = line_out[layer]
    forward_line(1)
    forward_plane(layer)
    for k in range(2, depth - 1):
        forward_line(k)
    signs(2, 6)
    forward_plane(others[0])
    signs(6, 9)
    for o in others[1:-1]:
        forward_plane(o)
    for o in others:
        head_line(o, o).wait_recv()
    plane_out[...] = jnp.sum(line_in[...], axis=0)

    def head_plane(d):
        to = me + steps[d]
        return send(
            plane_out.at[lax.rem(to // 2, 4)], plane_in.at[d], head_plane_send.at[d], head_plane_recv.at[d], to
        )

    for d in range(3):
        head_plane(d).start()
    signs(9, 12)
    for o in others[-1:]:
        forward_plane(o)
    signs(12, 16)
    for at_layer in [layer] + others:
        for r in range(4):
            to_partner(r, at_layer).wait()
        for d in range(3):
            in_plane(d, at_layer).wait_send()
    for o in others:
        along_line(o, layer).wait_send()
        head_line(o, o).wait_send()
    for d in range(3):
        head_plane(d).wait()

    last_items, last_sessions = all_ref[:, blocks - 1, :], all_ref[:, blocks + half - 1, :] >> 16
    next_items, next_sessions = all_ref[:, 0, :], all_ref[:, blocks, :] & 0xFFFF
    group = slabs // 4
    small = lax.broadcasted_iota(jnp.int32, (group, LANES), 1)

    def meet(last, following):
        joined = None
        for g in range(4):
            shift = 32 * g + 16
            pieces = (pltpu.roll(x[g * group : (g + 1) * group], shift % LANES, 1) for x in (last, following))
            both = jnp.where(lax.rem(small, 32) < 16, *pieces)
            joined = both if joined is None else jnp.where(small // 32 == g, both, joined)
        return joined

    slab_ids = lax.broadcasted_iota(jnp.int32, (slabs, LANES), 0)
    next_sessions = jnp.where(slab_ids == slabs - 1, -1, pltpu.roll(next_sessions, slabs - 1, 0))
    met_items = meet(last_items, pltpu.roll(next_items, slabs - 1, 0))
    met_sessions = meet(last_sessions, next_sessions)
    crossing = (sub // 32 == lane // 32) & ((lax.rem(sub, 32) < 16) != (lax.rem(lane, 32) < 16))
    crossing = crossing & (jnp.abs(sub - lane) <= WINDOW)
    extra = jnp.zeros((rows + 8, LANES), jnp.float32)
    extra_total = jnp.zeros((8, LANES), jnp.float32)
    for g in range(group):
        item, session = met_items[g : g + 1], met_sessions[g : g + 1]
        linked = one_where((jnp.broadcast_to(session, (LANES, LANES)).T == session) & crossing)
        hot = one_where(ids == item)
        links = jnp.dot(jnp.concatenate([hot, ones[:, 0:LANES]], axis=0), linked, preferred_element_type=jnp.float32)
        extra += lax.dot_general(links.astype(jnp.bfloat16), hot, NT, preferred_element_type=jnp.float32)
        extra_total += links[rows:]
    links_ref[...] = extra
    more = jnp.concatenate(
        [
            links_ref[pl.ds(me * share, share)],
            links_ref[rows : rows + 1],
            extra_total[0:1],
            jnp.zeros((6 - share, LANES), jnp.float32),
        ],
        axis=0,
    )
    head_ref[...] = plane_out[quad] + plane_in[0] + plane_in[1] + plane_in[2] + more


def take_windows(code_ref, length, start):
    whole, part = start >> 3, start & 7
    bits = max(1, (length // 8 - 1).bit_length())
    keep = 8 * ((1 << (bits - 1)) + 4)
    value = None
    for bit in reversed(range(bits)):
        step = 8 << bit
        keep = 8 * ((1 << bit) + 4)
        chosen = ((whole >> bit) & 1) == 1
        if value is None:
            low, high = code_ref[0:keep, :], code_ref[step : step + keep, :]
        else:
            low, high = value[0:keep], value[step : step + keep]
        value = jnp.where(chosen, high, low)
    for bit in (2, 1, 0):
        chosen = ((part >> bit) & 1) == 1
        value = jnp.where(chosen, pltpu.roll(value, value.shape[0] - (1 << bit), 0), value)
    return value[0:32]


def all_rows(value, combine):
    for shift in (4, 2, 1):
        value = combine(value, pltpu.roll(value, shift, 0))
    return value


def head_counts(window, ok, near, rows):
    center = window[16:17]
    linked = ((window ^ center) >> ITEM_BITS == 0) & near & ok
    item = window & ((1 << ITEM_BITS) - 1)
    tag = jnp.where(linked & (item < rows), item | rows, 0)
    packed = tag[0:8] | (tag[8:16] << 8) | (tag[16:24] << 16) | (tag[24:32] << 24)
    one = jnp.where(linked, 1, 0)
    weight = all_rows(one[0:8] + one[8:16] + one[16:24] + one[24:32], lambda x, y: x + y)
    sub = lax.broadcasted_iota(jnp.int32, (8, LANES), 0)

    def plane(k):
        spread = lax.shift_left(lax.shift_right_logical(packed, k) & 0x01010101, sub)
        return all_rows(spread, lambda x, y: x | y)

    bits = rows.bit_length() - 1
    node = plane(bits)
    for k in range(3):
        node = node & (plane(k) ^ (((sub >> k) & 1) - 1))
    nodes = [node]
    for k in reversed(range(3, bits)):
        word = plane(k)
        nodes = [part for node in nodes for part in (node & ~word, node & word)]
    counts = jnp.concatenate([lax.population_count(node).astype(jnp.float32) for node in nodes], axis=0)
    return counts.astype(jnp.bfloat16), weight[0:1].astype(jnp.float32), center & ((1 << ITEM_BITS) - 1)


def tile_kernel(rows, length, parts, base_ref, all_ref, count_ref, margin_ref, flat_ref, code_ref):
    item_mask = (1 << ITEM_BITS) - 1
    base = base_ref[0]
    count_ref[...] = jnp.zeros_like(count_ref)
    margin_ref[...] = jnp.zeros_like(margin_ref)
    width = count_ref.shape[2]
    band = parts * width
    slabs, blocks = all_ref.shape[0], all_ref.shape[1] * 2 // 3
    for n in range(slabs):
        paired = all_ref[n, blocks:]
        sessions = jnp.concatenate([paired & 0xFFFF, paired >> 16], axis=0)
        flat_ref[n * blocks : (n + 1) * blocks] = all_ref[n, 0:blocks] | (sessions << ITEM_BITS)
    per = length // LANES
    for r in range(per):
        code_ref[16 + r * LANES : 16 + (r + 1) * LANES] = flat_ref[pl.ds(r, LANES, stride=per), :].T
    lane = lax.broadcasted_iota(jnp.int32, (16, LANES), 1)
    code_ref[0:16] = jnp.where(lane == 0, -1, pltpu.roll(code_ref[length : length + 16], 1, 1))
    code_ref[length + 16 : length + 32] = jnp.where(
        lane == LANES - 1, -1, pltpu.roll(code_ref[16:32], LANES - 1, 1)
    )

    words = length // 32
    row_bit = jnp.left_shift(1, lax.broadcasted_iota(jnp.int32, (32, LANES), 0))
    masks = [[], []]
    for w in range(words):
        item = code_ref[16 + 32 * w : 48 + 32 * w] & item_mask
        for s in range(2):
            local = item - base - s * band
            mine = (local >= 0) & (local < band) & (item >= rows)
            masks[s].append(jnp.sum(jnp.where(mine, row_bit, 0), axis=0, keepdims=True))
    start_masks = tuple(jnp.concatenate(m, axis=0) for m in masks)
    tally = [jnp.sum(lax.population_count(m), axis=0, keepdims=True) for m in start_masks]
    trips = (jnp.max(jnp.maximum(tally[0], tally[1])) + 1) // 2

    word_ids = lax.broadcasted_iota(jnp.int32, (words, LANES), 0)
    d_ids = lax.broadcasted_iota(jnp.int32, (32, LANES), 0)
    near = (d_ids >= 1) & (d_ids != 16)
    tile = min(width, 256)
    t_ids = lax.broadcasted_iota(jnp.int32, (tile, 2 * LANES), 0).astype(jnp.float32).astype(jnp.bfloat16)
    p_ids = lax.broadcasted_iota(jnp.int32, (16, 2 * LANES), 0)

    def ends(mask):
        some = mask != 0
        first_row = jnp.min(jnp.where(some, word_ids, words), axis=0, keepdims=True)
        last_row = jnp.max(jnp.where(some, word_ids, -1), axis=0, keepdims=True)
        at_first, at_last = word_ids == first_row, word_ids == last_row
        first_word = jnp.sum(jnp.where(at_first, mask, 0), axis=0, keepdims=True)
        last_word = jnp.sum(jnp.where(at_last, mask, 0), axis=0, keepdims=True)
        first_bit = first_word & -first_word
        last_place = 31 - lax.clz(last_word)
        last_bit = jnp.where(last_word == 0, 0, jnp.left_shift(1, last_place & 31))
        first = 32 * first_row + lax.population_count(first_bit - 1)
        last = 32 * last_row + last_place
        first_ok = first_word != 0
        last_ok = first_ok & (last > first)
        mask = mask & ~(jnp.where(at_first, first_bit, 0) | jnp.where(at_last, last_bit, 0))
        return mask, ((first, first_ok), (last, last_ok))

    def body(unused, state):
        out = []
        for s in range(2):
            mask, found = ends(state[s])
            out.append(mask)
            links, weights, locals_ = [], [], []
            for at, ok in found:
                window = take_windows(code_ref, length, jnp.where(ok, at, 0))
                counts, weight, item = head_counts(window, ok, near, rows)
                links.append(counts)
                weights.append(weight)
                locals_.append(item - base - s * band)
            links = jnp.concatenate(links, axis=1)
            weight = jnp.concatenate(weights, axis=1)
            local = jnp.concatenate(locals_, axis=1)
            part = local >> (width.bit_length() - 1)
            inner = local & (width - 1)
            pieces = []
            for p in range(parts):
                chosen = jnp.broadcast_to(jnp.where(part == p, 1.0, 0.0), (16, 2 * LANES)).astype(jnp.bfloat16)
                pieces += [links[n : n + 16] * chosen for n in range(0, rows, 16)]
            pieces.append(jnp.where(p_ids == part, weight, 0.0).astype(jnp.bfloat16))
            left = jnp.concatenate(pieces, axis=0)
            for t in range(width // tile):
                inside = (inner >= t * tile) & (inner < (t + 1) * tile)
                hot = hot_columns(t_ids, jnp.where(inside, inner - t * tile, -1).astype(jnp.float32))
                cols = slice(t * tile, (t + 1) * tile)
                value = lax.dot_general(left, hot, NT, preferred_element_type=jnp.float32)
                count_ref[s, :, cols] += value[0 : parts * rows]
                margin_ref[s, :, cols] += value[parts * rows :]
        return tuple(out)

    lax.fori_loop(0, trips, body, start_masks)


def sign_table(words, width):
    size = words.shape[1]

    def wide(value):
        return jnp.concatenate([value] * (size // LANES), axis=1)

    shift = lax.broadcasted_iota(jnp.int32, (8, LANES), 0)
    parts = []
    for g in range(width // 8):
        word = 8 * g // BITS_PER_WORD
        split, offset = (word + 1) * BITS_PER_WORD - 8 * g, 8 * g - word * BITS_PER_WORD
        now = jnp.broadcast_to(words[word : word + 1], (8, size))
        where_bit = jnp.left_shift(1, shift + offset)
        if split < 8:
            later = jnp.broadcast_to(words[word + 1 : word + 2], (8, size))
            now = jnp.where(wide(shift) >= split, later, now)
            place = jnp.where(shift >= split, shift - split, shift + offset)
            where_bit = jnp.left_shift(1, place)
        parts.append(jnp.where((now & wide(where_bit)) != 0, 1.0, -1.0))
    return jnp.concatenate(parts, axis=0).astype(jnp.bfloat16)


def sketch_kernel(
    slabs, rows, parts, width, scale, count_ref, margin_ref, head_ref, sign_ref, bits_ref, out_ref,
    log_ref, head_bits, acc_ref, send_ref, recv_ref, bit_sem, send_sems, recv_sems,
):
    me = lax.axis_index("stream")
    barrier = greet_all(slabs, me)
    part = count_ref.shape[2]
    share = rows // slabs
    tile = min(part, 512)
    head_copy = pltpu.make_async_copy(bits_ref.at[:, 0:rows], head_bits, bit_sem.at[0])
    head_copy.start()

    log_ref[...] = jnp.log(jnp.maximum(margin_ref[...], 1.0))
    row_log = jnp.log(jnp.maximum(head_ref[share : share + 1], 1.0))
    column_log = jnp.broadcast_to(row_log, (rows, LANES)).T
    total_log = jnp.log(jnp.sum(head_ref[share + 1 : share + 2], axis=1, keepdims=True))
    row_term = total_log - column_log[:, 0:1]
    def product(positive, signs):
        upper = positive.astype(jnp.bfloat16)
        lower = (positive - upper.astype(jnp.float32)).astype(jnp.bfloat16)
        both = jnp.concatenate([upper, lower], axis=0)
        value = lax.dot_general(both, signs, NT, preferred_element_type=jnp.float32)
        return value[0:rows] + value[rows:]

    head_copy.wait()
    row = lax.broadcasted_iota(jnp.int32, (8, LANES), 0)
    shared = jnp.concatenate(
        [jnp.where(row < share, head_ref[...], 0.0), jnp.zeros((rows - 8, LANES), jnp.float32)], axis=0
    )
    shared = pltpu.roll(shared, me * share, 0)
    ratio = jnp.log(jnp.maximum(shared, 1.0)) + total_log - row_log - column_log
    first_band = jnp.where(lax.axis_index("item") == 0, 1.0, 0.0)
    positive = jnp.where(shared > 0, jnp.maximum(ratio, 0.0), 0.0) * first_band
    acc_ref[...] = product(positive.T, sign_table(head_bits[...], width))

    for s in range(2):
        for h in range(parts):
            for at in range(0, part, tile):
                counts = count_ref[s, h * rows : (h + 1) * rows, at : at + tile]
                ratio = jnp.log(jnp.maximum(counts, 1.0)) + row_term - log_ref[s, h : h + 1, at : at + tile]
                positive = jnp.where(counts > 0, jnp.maximum(ratio, 0.0), 0.0)
                bit_at = (s * parts + h) * part + at
                acc_ref[...] += product(positive, sign_ref[:, bit_at : bit_at + tile])

    cuts = width // LANES
    for d in range(slabs):
        for c in range(cuts):
            send_ref[d, c * share : (c + 1) * share] = (
                acc_ref[d * share : (d + 1) * share, c * LANES : (c + 1) * LANES] * scale
            )
    pl.semaphore_wait(barrier, slabs - 1)
    exchange(slabs, me, send_ref, recv_ref, send_sems, recv_sems, True)
    exchange(slabs, me, send_ref, recv_ref, send_sems, recv_sems, False)
    summed = jnp.sum(recv_ref[...], axis=0)
    out_ref[...] = jnp.concatenate([summed[c * share : (c + 1) * share] for c in range(cuts)], axis=1)


def local(event_items, event_sessions, sketch_bits):
    slabs = lax.axis_size("stream")
    slab = event_items.shape[0]
    total_events = slab * slabs
    words, band_size = sketch_bits.shape
    owned = band_size // slabs
    rows, width = 128, 256
    part = max(LANES, owned // 16)
    parts = owned // (2 * part)
    me = lax.axis_index("stream")
    own_start = me * owned
    first_id = lax.axis_index("item") * band_size + own_start
    blocks = slab // LANES
    length = total_events // LANES

    dma = pltpu.SemaphoreType.DMA
    depth = slabs // PLANE
    events, head, signs = pl.pallas_call(
        functools.partial(gather_kernel, slabs, rows, blocks),
        out_shape=(
            jax.ShapeDtypeStruct((slabs, blocks * 3 // 2, LANES), jnp.int32),
            jax.ShapeDtypeStruct((8, LANES), jnp.float32),
            jax.ShapeDtypeStruct((width, owned), jnp.bfloat16),
        ),
        in_specs=[VMEM, pl.BlockSpec(memory_space=pl.ANY)],
        out_specs=(VMEM, VMEM, VMEM),
        scratch_shapes=[
            pltpu.VMEM((blocks * 3 // 2, LANES), jnp.int32),
            pltpu.VMEM((words, owned), jnp.int32),
            pltpu.VMEM((blocks + 16, LANES), jnp.int32),
            pltpu.VMEM((blocks + 16, LANES), jnp.int32),
            pltpu.VMEM((rows + 8, LANES), jnp.float32),
            pltpu.VMEM((8, LANES), jnp.float32),
            pltpu.VMEM((2, depth, 4, 8, LANES), jnp.float32),
            pltpu.VMEM((depth, 4, 8, LANES), jnp.float32),
            pltpu.VMEM((4, 8, LANES), jnp.float32),
            pltpu.VMEM((3, 8, LANES), jnp.float32),
            pltpu.VMEM((depth, 4, 8, LANES), jnp.float32),
            pltpu.VMEM((depth, 4, 8, LANES), jnp.float32),
            dma((1,)),
            dma((depth,)),
            dma((depth,)),
            dma((3 * depth,)),
            dma((3 * depth,)),
            dma((4 * depth,)),
            dma((4 * depth,)),
            dma((2,)),
            dma((3,)),
            dma((3,)),
            dma((depth,)),
            dma((depth,)),
        ],
        compiler_params=pltpu.CompilerParams(
            collective_id=0, has_side_effects=True, vmem_limit_bytes=VMEM_GRANT
        ),
        name="gather_events",
    )(jnp.stack([event_items, event_sessions]).reshape(2, blocks, LANES), sketch_bits)

    counts, margins = pl.pallas_call(
        functools.partial(tile_kernel, rows, length, parts),
        out_shape=(
            jax.ShapeDtypeStruct((2, parts * rows, part), jnp.float32),
            jax.ShapeDtypeStruct((2, 16, part), jnp.float32),
        ),
        in_specs=[pl.BlockSpec(memory_space=pltpu.SMEM), VMEM],
        out_specs=(VMEM, VMEM),
        scratch_shapes=[
            pltpu.VMEM((length, LANES), jnp.int32),
            pltpu.VMEM((length + 32, LANES), jnp.int32),
        ],
        compiler_params=pltpu.CompilerParams(vmem_limit_bytes=VMEM_GRANT),
        name="tile_counts",
    )(first_id.astype(jnp.int32)[None], events)

    own_rows = pl.pallas_call(
        functools.partial(sketch_kernel, slabs, rows, parts, width, 1.0 / math.sqrt(total_events)),
        out_shape=jax.ShapeDtypeStruct((rows // slabs, width), jnp.float32),
        in_specs=[VMEM] * 4 + [pl.BlockSpec(memory_space=pl.ANY)],
        out_specs=VMEM,
        scratch_shapes=[
            pltpu.VMEM((2, 16, part), jnp.float32),
            pltpu.VMEM((words, rows), jnp.int32),
            pltpu.VMEM((rows, width), jnp.float32),
            pltpu.VMEM((slabs, 8, LANES), jnp.float32),
            pltpu.VMEM((slabs, 8, LANES), jnp.float32),
            dma((1,)),
            dma((slabs,)),
            dma((slabs,)),
        ],
        compiler_params=pltpu.CompilerParams(
            collective_id=1, has_side_effects=True, vmem_limit_bytes=VMEM_GRANT
        ),
        name="sketch_tile",
    )(counts, margins, head, signs, sketch_bits)
    if lax.axis_size("item") > 1:
        own_rows = lax.psum(own_rows, "item")
    return own_rows


def solution(mesh):
    placed = (P("stream"), P("stream"), P(None, "item"))
    return jax.shard_map(
        local, mesh=mesh, in_specs=placed, out_specs=P("stream", None), check_vma=False
    )
```

profile of v0, /device:TPU:0, one launch (start us, length us, event | category | flops | bytes accessed | tf_op | source)
XLA Modules:
  0.0 38.4 jit_solution(15124106124976340323)
XLA Ops:
  0.0 0.7 %pad_add_fusion.own_ref = s32[2,32,128]{2,1,0:T(8,128)S(1)} fusion(s32[1,32,128]{2,1,0:T(8,128)} %bitcast.3, s32[1,32,128]{2,1,0:T(8,128)} %bitcast.4), kind=kLoop, calls=%fused_computation | loop fusion | flops 8192 | bytes 65536 | tf_op jit(solution)/shard_map/stack | solution.py:587
  0.7 19.2 %gather_events.1 = (s32[32,48,128]{2,1,0:T(8,128)S(1)}, f32[8,128]{1,0:T(8,128)S(1)}, bf16[256,8192]{1,0:T(8,128)(2,1)S(1)}) custom-call(s32[2,32,128]{2,1,0:T(8,128)S(1)} %pad_add_fusion.own_ref, s32[15,262144]{1,0:T(8,128)} %bits_ref.3), custom_call_target="tpu_custom_call" | custom-call | tf_op jit(solution)/shard_map/gather_events/pallas_call | solution.py:548
  20.0 8.6 %tile_counts.1 = (f32[2,1024,512]{2,1,0:T(8,128)S(1)}, f32[2,16,512]{2,1,0:T(8,128)S(1)}) custom-call(s32[1]{0:T(128)} %bitcast.base_ref, s32[32,48,128]{2,1,0:T(8,128)S(1)} %get-tuple-element.10.all_ref), custom_call_target="tpu_custom_call" | custom-call | tf_op jit(solution)/shard_map/tile_counts/pallas_call | solution.py:589
  28.6 9.2 %sketch_tile.1 = f32[4,256]{1,0:T(4,128)S(1)} custom-call(f32[2,1024,512]{2,1,0:T(8,128)S(1)} %get-tuple-element.11.count_ref, f32[2,16,512]{2,1,0:T(8,128)S(1)} %get-tuple-element.12.margin_ref, f32[8,128]{1,0:T(8,128)S(1)} %get-tuple-element.13.head_ref, bf16[256,8192]{1,0:T(8,128)(2,1)S(1)} %get-tuple-element.14.sign_ref, s32[15,262144]{1,0:T(8,128)} %bits_ref.3), custom_call_target="tpu_custom_call" | custom-call | tf_op jit(solution)/shard_map/sketch_tile/pallas_call | solution.py:605
  37.8 0.6 %copy.5 = f32[4,256]{1,0:T(4,128)} copy(f32[4,256]{1,0:T(4,128)S(1)} %sketch_tile.1) | data formatting | bytes 8192
where the time goes:
time: 39.1 us; the launch traced here: 38.4 us
  Pallas kernels  37.1 us (95%)
  other arithmetic  0.74 us (2%)
  local copies, waits for them, and re-layouts  0.6 us (2%)
    pallas_call x1, Pallas kernels, local(): pl.pallas_call(functools.partial(gather_kernel, slabs, rows, blocks), out...  19.2 us
    pallas_call x1, Pallas kernels, local(): pl.pallas_call(functools.partial(sketch_kernel, slabs, rows, parts, width...  9.19 us
    pallas_call x1, Pallas kernels, local(): pl.pallas_call(functools.partial(tile_kernel, rows, length, parts), out_s...  8.62 us

commit v1 on v0

--- a/solution.py
+++ b/solution.py
@@ -13,6 +13,7 @@
 LANES = 128
 BITS_PER_WORD = 18
 PLANE = 8
+BANDS = 4
 VMEM_GRANT = 45 * 1024 * 1024
 NT = (((1,), (1,)), ((), ()))
 VMEM = pl.BlockSpec(memory_space=pltpu.VMEM)
@@ -148,7 +149,7 @@
         total_ref[...] += links[rows:]
         return unused
 
-    inner = [blocks * n // 32 for n in (0, 16, 32)]
+    inner = [blocks * n // 32 for n in (0, 8, 28, 32)]
 
     def blocks_of(n):
         lax.fori_loop(inner[n], inner[n + 1], block, 0, unroll=4)
@@ -201,6 +202,8 @@
             to_partner(d + 1, at_layer).start()
 
     blocks_of(1)
+    forward_line(0)
+    blocks_of(2)
     share = rows // slabs
     tail = jnp.concatenate(
         [links_ref[rows : rows + 1], total_ref[0:1], jnp.zeros((6 - share, LANES), jnp.float32)], axis=0
@@ -212,8 +215,8 @@
 
     pair = send(pair_out.at[1 - parity], pair_in, pair_sems.at[0], pair_sems.at[1], partner)
     pair.start()
+    forward_line(1)
     signs(0, 2)
-    forward_line(0)
     pair.wait()
     line_out[...] = pair_out[parity] + pair_in[...]
 
@@ -226,7 +229,6 @@
     for o in others:
         head_line(o, layer).start()
     line_in[layer] = line_out[layer]
-    forward_line(1)
     forward_plane(layer)
     for k in range(2, depth - 1):
         forward_line(k)
@@ -261,47 +263,7 @@
         head_line(o, o).wait_send()
     for d in range(3):
         head_plane(d).wait()
-
-    last_items, last_sessions = all_ref[:, blocks - 1, :], all_ref[:, blocks + half - 1, :] >> 16
-    next_items, next_sessions = all_ref[:, 0, :], all_ref[:, blocks, :] & 0xFFFF
-    group = slabs // 4
-    small = lax.broadcasted_iota(jnp.int32, (group, LANES), 1)
-
-    def meet(last, following):
-        joined = None
-        for g in range(4):
-            shift = 32 * g + 16
-            pieces = (pltpu.roll(x[g * group : (g + 1) * group], shift % LANES, 1) for x in (last, following))
-            both = jnp.where(lax.rem(small, 32) < 16, *pieces)
-            joined = both if joined is None else jnp.where(small // 32 == g, both, joined)
-        return joined
-
-    slab_ids = lax.broadcasted_iota(jnp.int32, (slabs, LANES), 0)
-    next_sessions = jnp.where(slab_ids == slabs - 1, -1, pltpu.roll(next_sessions, slabs - 1, 0))
-    met_items = meet(last_items, pltpu.roll(next_items, slabs - 1, 0))
-    met_sessions = meet(last_sessions, next_sessions)
-    crossing = (sub // 32 == lane // 32) & ((lax.rem(sub, 32) < 16) != (lax.rem(lane, 32) < 16))
-    crossing = crossing & (jnp.abs(sub - lane) <= WINDOW)
-    extra = jnp.zeros((rows + 8, LANES), jnp.float32)
-    extra_total = jnp.zeros((8, LANES), jnp.float32)
-    for g in range(group):
-        item, session = met_items[g : g + 1], met_sessions[g : g + 1]
-        linked = one_where((jnp.broadcast_to(session, (LANES, LANES)).T == session) & crossing)
-        hot = one_where(ids == item)
-        links = jnp.dot(jnp.concatenate([hot, ones[:, 0:LANES]], axis=0), linked, preferred_element_type=jnp.float32)
-        extra += lax.dot_general(links.astype(jnp.bfloat16), hot, NT, preferred_element_type=jnp.float32)
-        extra_total += links[rows:]
-    links_ref[...] = extra
-    more = jnp.concatenate(
-        [
-            links_ref[pl.ds(me * share, share)],
-            links_ref[rows : rows + 1],
-            extra_total[0:1],
-            jnp.zeros((6 - share, LANES), jnp.float32),
-        ],
-        axis=0,
-    )
-    head_ref[...] = plane_out[quad] + plane_in[0] + plane_in[1] + plane_in[2] + more
+    head_ref[...] = plane_out[quad] + plane_in[0] + plane_in[1] + plane_in[2]
 
 
 def take_windows(code_ref, length, start):
@@ -330,19 +292,28 @@
     return value
 
 
+def bytes_of_rows(tag):
+    return tag[0:8] | (tag[8:16] << 8) | (tag[16:24] << 16) | (tag[24:32] << 24)
+
+
+def plane_word(packed, k):
+    sub = lax.broadcasted_iota(jnp.int32, (8, LANES), 0)
+    spread = lax.shift_left(lax.shift_right_logical(packed, k) & 0x01010101, sub)
+    return all_rows(spread, lambda x, y: x | y)
+
+
 def head_counts(window, ok, near, rows):
     center = window[16:17]
     linked = ((window ^ center) >> ITEM_BITS == 0) & near & ok
     item = window & ((1 << ITEM_BITS) - 1)
     tag = jnp.where(linked & (item < rows), item | rows, 0)
-    packed = tag[0:8] | (tag[8:16] << 8) | (tag[16:24] << 16) | (tag[24:32] << 24)
+    packed = bytes_of_rows(tag)
     one = jnp.where(linked, 1, 0)
     weight = all_rows(one[0:8] + one[8:16] + one[16:24] + one[24:32], lambda x, y: x + y)
     sub = lax.broadcasted_iota(jnp.int32, (8, LANES), 0)
 
     def plane(k):
-        spread = lax.shift_left(lax.shift_right_logical(packed, k) & 0x01010101, sub)
-        return all_rows(spread, lambda x, y: x | y)
+        return plane_word(packed, k)
 
     bits = rows.bit_length() - 1
     node = plane(bits)
@@ -356,12 +327,12 @@
     return counts.astype(jnp.bfloat16), weight[0:1].astype(jnp.float32), center & ((1 << ITEM_BITS) - 1)
 
 
-def tile_kernel(rows, length, parts, base_ref, all_ref, count_ref, margin_ref, flat_ref, code_ref):
+def tile_kernel(rows, length, parts, base_ref, all_ref, count_ref, margin_ref, flat_ref, code_ref, mask_ref):
     item_mask = (1 << ITEM_BITS) - 1
     base = base_ref[0]
     count_ref[...] = jnp.zeros_like(count_ref)
     margin_ref[...] = jnp.zeros_like(margin_ref)
-    width = count_ref.shape[2]
+    bands, unused_rows, width = count_ref.shape
     band = parts * width
     slabs, blocks = all_ref.shape[0], all_ref.shape[1] * 2 // 3
     for n in range(slabs):
@@ -378,17 +349,24 @@
     )
 
     words = length // 32
-    row_bit = jnp.left_shift(1, lax.broadcasted_iota(jnp.int32, (32, LANES), 0))
-    masks = [[], []]
+    band_bits = (bands - 1).bit_length()
     for w in range(words):
         item = code_ref[16 + 32 * w : 48 + 32 * w] & item_mask
-        for s in range(2):
-            local = item - base - s * band
-            mine = (local >= 0) & (local < band) & (item >= rows)
-            masks[s].append(jnp.sum(jnp.where(mine, row_bit, 0), axis=0, keepdims=True))
-    start_masks = tuple(jnp.concatenate(m, axis=0) for m in masks)
-    tally = [jnp.sum(lax.population_count(m), axis=0, keepdims=True) for m in start_masks]
-    trips = (jnp.max(jnp.maximum(tally[0], tally[1])) + 1) // 2
+        local = item - base
+        mine = (local >= 0) & (local < bands * band) & (item >= rows)
+        packed = bytes_of_rows(jnp.where(mine, (local >> (band.bit_length() - 1)) | bands, 0))
+        for k in range(band_bits + 1):
+            mask_ref[k, w : w + 1] = plane_word(packed, k)[0:1]
+    planes = [mask_ref[k] for k in range(band_bits + 1)]
+    for s in range(bands):
+        mask = planes[band_bits]
+        for k in range(band_bits):
+            mask = mask & (planes[k] if s >> k & 1 else ~planes[k])
+        mask_ref[s] = mask
+    bounds = []
+    for s in range(bands):
+        tally = jnp.sum(lax.population_count(mask_ref[s]), axis=0, keepdims=True)
+        bounds.append((jnp.max(tally) + 1) // 2 + (bounds[-1] if bounds else 0))
 
     word_ids = lax.broadcasted_iota(jnp.int32, (words, LANES), 0)
     d_ids = lax.broadcasted_iota(jnp.int32, (32, LANES), 0)
@@ -414,39 +392,46 @@
         mask = mask & ~(jnp.where(at_first, first_bit, 0) | jnp.where(at_last, last_bit, 0))
         return mask, ((first, first_ok), (last, last_ok))
 
-    def body(unused, state):
-        out = []
-        for s in range(2):
-            mask, found = ends(state[s])
-            out.append(mask)
-            links, weights, locals_ = [], [], []
-            for at, ok in found:
-                window = take_windows(code_ref, length, jnp.where(ok, at, 0))
-                counts, weight, item = head_counts(window, ok, near, rows)
-                links.append(counts)
-                weights.append(weight)
-                locals_.append(item - base - s * band)
-            links = jnp.concatenate(links, axis=1)
-            weight = jnp.concatenate(weights, axis=1)
-            local = jnp.concatenate(locals_, axis=1)
-            part = local >> (width.bit_length() - 1)
-            inner = local & (width - 1)
-            pieces = []
-            for p in range(parts):
-                chosen = jnp.broadcast_to(jnp.where(part == p, 1.0, 0.0), (16, 2 * LANES)).astype(jnp.bfloat16)
-                pieces += [links[n : n + 16] * chosen for n in range(0, rows, 16)]
-            pieces.append(jnp.where(p_ids == part, weight, 0.0).astype(jnp.bfloat16))
-            left = jnp.concatenate(pieces, axis=0)
-            for t in range(width // tile):
-                inside = (inner >= t * tile) & (inner < (t + 1) * tile)
-                hot = hot_columns(t_ids, jnp.where(inside, inner - t * tile, -1).astype(jnp.float32))
-                cols = slice(t * tile, (t + 1) * tile)
-                value = lax.dot_general(left, hot, NT, preferred_element_type=jnp.float32)
-                count_ref[s, :, cols] += value[0 : parts * rows]
-                margin_ref[s, :, cols] += value[parts * rows :]
-        return tuple(out)
-
-    lax.fori_loop(0, trips, body, start_masks)
+    def find(s):
+        mask, found = ends(mask_ref[s])
+        mask_ref[s] = mask
+        links, weights, locals_ = [], [], []
+        for at, ok in found:
+            window = take_windows(code_ref, length, jnp.where(ok, at, 0))
+            counts, weight, item = head_counts(window, ok, near, rows)
+            links.append(counts)
+            weights.append(weight)
+            locals_.append(item - base - s * band)
+        return tuple(jnp.concatenate(x, axis=1) for x in (links, weights, locals_))
+
+    def count(s, links, weight, local):
+        part = local >> (width.bit_length() - 1)
+        inner = local & (width - 1)
+        pieces = []
+        for p in range(parts):
+            chosen = jnp.broadcast_to(jnp.where(part == p, 1.0, 0.0), (16, 2 * LANES)).astype(jnp.bfloat16)
+            pieces += [links[n : n + 16] * chosen for n in range(0, rows, 16)]
+        pieces.append(jnp.where(p_ids == part, weight, 0.0).astype(jnp.bfloat16))
+        left = jnp.concatenate(pieces, axis=0)
+        for t in range(width // tile):
+            inside = (inner >= t * tile) & (inner < (t + 1) * tile)
+            hot = hot_columns(t_ids, jnp.where(inside, inner - t * tile, -1).astype(jnp.float32))
+            cols = slice(t * tile, (t + 1) * tile)
+            value = lax.dot_general(left, hot, NT, preferred_element_type=jnp.float32)
+            count_ref[s, :, cols] += value[0 : parts * rows]
+            margin_ref[s, :, cols] += value[parts * rows :]
+
+    def band_of(trip):
+        s = jnp.int32(0)
+        for bound in bounds[:-1]:
+            s += jnp.where(trip >= bound, 1, 0)
+        return s
+
+    def body(trip, found):
+        count(band_of(trip), *found)
+        return find(band_of(trip + 1))
+
+    lax.fori_loop(0, bounds[-1], body, find(band_of(0)))
 
 
 def sign_table(words, width):
@@ -471,22 +456,70 @@
     return jnp.concatenate(parts, axis=0).astype(jnp.bfloat16)
 
 
+def boundary_counts(rows, share, me, all_ref, extra_ref):
+    slabs, blocks = all_ref.shape[0], all_ref.shape[1] * 2 // 3
+    half = blocks // 2
+    group = slabs // 4
+    sub = lax.broadcasted_iota(jnp.int32, (LANES, LANES), 0)
+    lane = lax.broadcasted_iota(jnp.int32, (LANES, LANES), 1)
+    ids = lax.broadcasted_iota(jnp.int32, (rows, LANES), 0)
+    small = lax.broadcasted_iota(jnp.int32, (group, LANES), 1)
+    last_items, last_sessions = all_ref[:, blocks - 1, :], all_ref[:, blocks + half - 1, :] >> 16
+    next_items, next_sessions = all_ref[:, 0, :], all_ref[:, blocks, :] & 0xFFFF
+
+    def meet(last, following):
+        joined = None
+        for g in range(4):
+            shift = 32 * g + 16
+            pieces = (pltpu.roll(x[g * group : (g + 1) * group], shift, 1) for x in (last, following))
+            both = jnp.where(small % 32 < 16, *pieces)
+            joined = both if joined is None else jnp.where(small // 32 == g, both, joined)
+        return joined
+
+    slab_ids = lax.broadcasted_iota(jnp.int32, (slabs, LANES), 0)
+    next_sessions = jnp.where(slab_ids == slabs - 1, -1, pltpu.roll(next_sessions, slabs - 1, 0))
+    met_items = meet(last_items, pltpu.roll(next_items, slabs - 1, 0))
+    met_sessions = meet(last_sessions, next_sessions)
+    crossing = ((sub >> 5) == (lane >> 5)) & (((sub ^ lane) & 16) != 0) & (jnp.abs(sub - lane) <= WINDOW)
+    ones = jnp.ones((8, LANES), jnp.float32).astype(jnp.bfloat16)
+    extra = jnp.zeros((rows + 8, LANES), jnp.float32)
+    total = jnp.zeros((8, LANES), jnp.float32)
+    for g in range(group):
+        item, session = met_items[g : g + 1], met_sessions[g : g + 1]
+        linked = one_where((jnp.broadcast_to(session, (LANES, LANES)).T == session) & crossing)
+        hot = one_where(ids == item)
+        links = jnp.dot(jnp.concatenate([hot, ones], axis=0), linked, preferred_element_type=jnp.float32)
+        extra += lax.dot_general(links.astype(jnp.bfloat16), hot, NT, preferred_element_type=jnp.float32)
+        total += links[rows:]
+    extra_ref[...] = extra
+    return jnp.concatenate(
+        [
+            extra_ref[pl.ds(me * share, share)],
+            extra_ref[rows : rows + 1],
+            total[0:1],
+            jnp.zeros((6 - share, LANES), jnp.float32),
+        ],
+        axis=0,
+    )
+
+
 def sketch_kernel(
-    slabs, rows, parts, width, scale, count_ref, margin_ref, head_ref, sign_ref, bits_ref, out_ref,
-    log_ref, head_bits, acc_ref, send_ref, recv_ref, bit_sem, send_sems, recv_sems,
+    slabs, rows, parts, width, scale, count_ref, margin_ref, head_ref, sign_ref, all_ref, bits_ref, out_ref,
+    extra_ref, log_ref, head_bits, acc_ref, send_ref, recv_ref, bit_sem, send_sems, recv_sems,
 ):
     me = lax.axis_index("stream")
     barrier = greet_all(slabs, me)
-    part = count_ref.shape[2]
+    bands, unused_rows, part = count_ref.shape
     share = rows // slabs
     tile = min(part, 512)
     head_copy = pltpu.make_async_copy(bits_ref.at[:, 0:rows], head_bits, bit_sem.at[0])
     head_copy.start()
 
     log_ref[...] = jnp.log(jnp.maximum(margin_ref[...], 1.0))
-    row_log = jnp.log(jnp.maximum(head_ref[share : share + 1], 1.0))
+    head = head_ref[...] + boundary_counts(rows, share, me, all_ref, extra_ref)
+    row_log = jnp.log(jnp.maximum(head[share : share + 1], 1.0))
     column_log = jnp.broadcast_to(row_log, (rows, LANES)).T
-    total_log = jnp.log(jnp.sum(head_ref[share + 1 : share + 2], axis=1, keepdims=True))
+    total_log = jnp.log(jnp.sum(head[share + 1 : share + 2], axis=1, keepdims=True))
     row_term = total_log - column_log[:, 0:1]
     def product(positive, signs):
         upper = positive.astype(jnp.bfloat16)
@@ -498,7 +531,7 @@
     head_copy.wait()
     row = lax.broadcasted_iota(jnp.int32, (8, LANES), 0)
     shared = jnp.concatenate(
-        [jnp.where(row < share, head_ref[...], 0.0), jnp.zeros((rows - 8, LANES), jnp.float32)], axis=0
+        [jnp.where(row < share, head, 0.0), jnp.zeros((rows - 8, LANES), jnp.float32)], axis=0
     )
     shared = pltpu.roll(shared, me * share, 0)
     ratio = jnp.log(jnp.maximum(shared, 1.0)) + total_log - row_log - column_log
@@ -506,7 +539,7 @@
     positive = jnp.where(shared > 0, jnp.maximum(ratio, 0.0), 0.0) * first_band
     acc_ref[...] = product(positive.T, sign_table(head_bits[...], width))
 
-    for s in range(2):
+    for s in range(bands):
         for h in range(parts):
             for at in range(0, part, tile):
                 counts = count_ref[s, h * rows : (h + 1) * rows, at : at + tile]
@@ -536,7 +569,8 @@
     owned = band_size // slabs
     rows, width = 128, 256
     part = max(LANES, owned // 16)
-    parts = owned // (2 * part)
+    bands = BANDS
+    parts = owned // (bands * part)
     me = lax.axis_index("stream")
     own_start = me * owned
     first_id = lax.axis_index("item") * band_size + own_start
@@ -589,14 +623,15 @@
     counts, margins = pl.pallas_call(
         functools.partial(tile_kernel, rows, length, parts),
         out_shape=(
-            jax.ShapeDtypeStruct((2, parts * rows, part), jnp.float32),
-            jax.ShapeDtypeStruct((2, 16, part), jnp.float32),
+            jax.ShapeDtypeStruct((bands, parts * rows, part), jnp.float32),
+            jax.ShapeDtypeStruct((bands, 16, part), jnp.float32),
         ),
         in_specs=[pl.BlockSpec(memory_space=pltpu.SMEM), VMEM],
         out_specs=(VMEM, VMEM),
         scratch_shapes=[
             pltpu.VMEM((length, LANES), jnp.int32),
             pltpu.VMEM((length + 32, LANES), jnp.int32),
+            pltpu.VMEM((bands, length // 32, LANES), jnp.int32),
         ],
         compiler_params=pltpu.CompilerParams(vmem_limit_bytes=VMEM_GRANT),
         name="tile_counts",
@@ -605,10 +640,11 @@
     own_rows = pl.pallas_call(
         functools.partial(sketch_kernel, slabs, rows, parts, width, 1.0 / math.sqrt(total_events)),
         out_shape=jax.ShapeDtypeStruct((rows // slabs, width), jnp.float32),
-        in_specs=[VMEM] * 4 + [pl.BlockSpec(memory_space=pl.ANY)],
+        in_specs=[VMEM] * 5 + [pl.BlockSpec(memory_space=pl.ANY)],
         out_specs=VMEM,
         scratch_shapes=[
-            pltpu.VMEM((2, 16, part), jnp.float32),
+            pltpu.VMEM((rows + 8, LANES), jnp.float32),
+            pltpu.VMEM((bands, 16, part), jnp.float32),
             pltpu.VMEM((words, rows), jnp.int32),
             pltpu.VMEM((rows, width), jnp.float32),
             pltpu.VMEM((slabs, 8, LANES), jnp.float32),
@@ -621,7 +657,7 @@
             collective_id=1, has_side_effects=True, vmem_limit_bytes=VMEM_GRANT
         ),
         name="sketch_tile",
-    )(counts, margins, head, signs, sketch_bits)
+    )(counts, margins, head, signs, events, sketch_bits)
     if lax.axis_size("item") > 1:
         own_rows = lax.psum(own_rows, "item")
     return own_rows

time: 39.1 us -> 39.4 us (level); the launches traced: 38.4 us -> 39.1 us
  Pallas kernels: 37.1 us -> 37.8 us
    pallas_call x1, Pallas kernels: 8.62 us -> 9.73 us  [local(): pl.pallas_call(functools.partial(tile_kernel, rows, length, parts), out_s...]
    pallas_call x1, Pallas kernels: 19.2 us -> 18.4 us  [local(): pl.pallas_call(functools.partial(gather_kernel, slabs, rows, blocks), out...]
    pallas_call x1, Pallas kernels: 9.19 us -> 9.64 us  [local(): pl.pallas_call(functools.partial(sketch_kernel, slabs, rows, parts, width...]
where the time goes in v1:
time: 39.4 us; the launch traced here: 39.1 us
  Pallas kernels  37.8 us (96%)
  other arithmetic  0.74 us (2%)
  local copies, waits for them, and re-layouts  0.6 us (2%)
    pallas_call x1, Pallas kernels, local(): pl.pallas_call(functools.partial(gather_kernel, slabs, rows, blocks), out...  18.4 us
    pallas_call x1, Pallas kernels, local(): pl.pallas_call(functools.partial(tile_kernel, rows, length, parts), out_s...  9.73 us
    pallas_call x1, Pallas kernels, local(): pl.pallas_call(functools.partial(sketch_kernel, slabs, rows, parts, width...  9.64 us

profile of v1, /device:TPU:0, one launch (start us, length us, event | category | flops | bytes accessed | tf_op | source)
XLA Modules:
  0.0 39.1 jit_solution(13909255259341388506)
XLA Ops:
  0.0 0.7 %pad_add_fusion.own_ref = s32[2,32,128]{2,1,0:T(8,128)S(1)} fusion(s32[1,32,128]{2,1,0:T(8,128)} %bitcast.3, s32[1,32,128]{2,1,0:T(8,128)} %bitcast.4), kind=kLoop, calls=%fused_computation | loop fusion | flops 8192 | bytes 65536 | tf_op jit(solution)/shard_map/stack | solution.py:621
  0.7 18.4 %gather_events.1 = (s32[32,48,128]{2,1,0:T(8,128)S(1)}, f32[8,128]{1,0:T(8,128)S(1)}, bf16[256,8192]{1,0:T(8,128)(2,1)S(1)}) custom-call(s32[2,32,128]{2,1,0:T(8,128)S(1)} %pad_add_fusion.own_ref, s32[15,262144]{1,0:T(8,128)} %bits_ref.3), custom_call_target="tpu_custom_call" | custom-call | tf_op jit(solution)/shard_map/gather_events/pallas_call | solution.py:582
  19.1 9.7 %tile_counts.1 = (f32[4,512,512]{2,1,0:T(8,128)S(1)}, f32[4,16,512]{2,1,0:T(8,128)S(1)}) custom-call(s32[1]{0:T(128)} %bitcast.base_ref, s32[32,48,128]{2,1,0:T(8,128)S(1)} %get-tuple-element.10.all_ref), custom_call_target="tpu_custom_call" | custom-call | tf_op jit(solution)/shard_map/tile_counts/pallas_call | solution.py:623
  28.9 9.6 %sketch_tile.1 = f32[4,256]{1,0:T(4,128)S(1)} custom-call(f32[4,512,512]{2,1,0:T(8,128)S(1)} %get-tuple-element.11.count_ref, f32[4,16,512]{2,1,0:T(8,128)S(1)} %get-tuple-element.12.margin_ref, f32[8,128]{1,0:T(8,128)S(1)} %get-tuple-element.13.head_ref, bf16[256,8192]{1,0:T(8,128)(2,1)S(1)} %get-tuple-element.14.sign_ref, ...), custom_call_target="tpu_custom_call" | custom-call | tf_op jit(solution)/shard_map/sketch_tile/pallas_call | solution.py:640
  38.5 0.6 %copy.5 = f32[4,256]{1,0:T(4,128)} copy(f32[4,256]{1,0:T(4,128)S(1)} %sketch_tile.1) | data formatting | bytes 8192
